TPU v7x, 32 devices: a whole 2x2x4 slice. The times are simulated.
32 devices in a mesh: blk: 8 (over z, y), layer: 4 (over x, core).
Axes of the slice: x: 2, y: 2, z: 4, core: 2. Of those that a mesh axis runs over, the one named last changes fastest.
Arguments:
- leaf_area: float32 [12, 16, 1024], P(None, 'layer', 'blk'), may hold values from 0 to 6
- soil_water: float32 [10, 1024], P(None, 'blk'), may hold values from 0.05 to 0.5
- root_share: float32 [16, 10], P('layer'), may hold values from 0 to 0.3
- patch_weight: float32 [16, 32768], P('layer', 'blk'), may hold values from 0 to 1
- patch_owner: int32 [32768, 1], P('blk'), may hold values from 0 to 7; in each aligned block of 4096 rows (0 to 4095, 4096 to 8191, ...) at most 1024 rows name the same one
- patch_local: int32 [32768], P('blk'), may hold values from 0 to 127
- month: int32 [1], replicated, may hold values from 0 to 11
- mix: float32 [1], replicated, may hold values from 0.1 to 0.9
Outputs:
- canopy_share: float32 [16, 1024], P('layer', 'blk')
Inputs may be any that keep to these rules, and one draw needn't show every extreme that they name: `patch_owner`: among the rows of one device, no owner is named more than 1024 times, a bound that some block reaches.
All inputs are finite; a program needn't handle non-finite values.
Results may differ from a plain program's by a relative error of at most 0.000065.
Values sent between devices are 32-bit elements; how exact they have to be, the bound alone decides.
A program may use at most 64 MiB of HBM per device.

v0:
```python
import functools

import jax
import jax.numpy as jnp
from jax import lax
from jax.experimental import pallas as pl
from jax.experimental.pallas import tpu as pltpu
from jax.sharding import PartitionSpec as P

MESH = pl.DeviceIdType.MESH
CHUNK = 512


def local_sums(weight, owner, local, owners, cells):
    types, patches = weight.shape
    chunk = CHUNK if patches % CHUNK == 0 else patches
    row_owner = lax.broadcasted_iota(jnp.int32, (owners * types, chunk), 0) // types
    cell = lax.broadcasted_iota(jnp.int32, (cells, chunk), 0)
    total = None
    for start in range(0, patches, chunk):
        part = slice(start, start + chunk)
        w = weight[:, part]
        high = w.astype(jnp.bfloat16).astype(jnp.float32)
        low = w - high
        named = row_owner == owner[:, part]
        left = jnp.concatenate(
            [
                jnp.where(named, jnp.concatenate([piece] * owners, axis=0), 0.0)
                for piece in (high, low)
            ],
            axis=0,
        ).astype(jnp.bfloat16)
        table = jnp.where(cell == local[:, part], 1.0, 0.0).astype(jnp.bfloat16)
        product = lax.dot_general(
            left, table, (((1,), (1,)), ((), ())), preferred_element_type=jnp.float32
        )
        total = product if total is None else total + product
    return total[: owners * types] + total[owners * types :]


def kernel(
    n, m, leaf_hbm, soil_hbm, root_hbm, weight_hbm, owner_hbm, local_hbm, month_hbm, mix_hbm,
    out_ref, leaf, soil, root, weight, owner, local, month, mix,
    sums, pair, got_sums, got_pairs, load_sem, send_sem, recv_sem,
):
    blk, layer = lax.axis_index("blk"), lax.axis_index("layer")
    types, cells = out_ref.shape
    loads = [
        pltpu.make_async_copy(source, target, load_sem.at[i])
        for i, (source, target) in enumerate(
            (
                (weight_hbm, weight),
                (owner_hbm, owner),
                (local_hbm, local),
                (month_hbm, month),
                (mix_hbm, mix),
                (leaf_hbm, leaf),
                (soil_hbm, soil),
                (root_hbm, root),
            )
        )
    ]
    for load in loads:
        load.start()

    def device(step_blk, step_layer):
        return (lax.rem(blk + step_blk, n), lax.rem(layer + step_layer, m))

    steps = [(i, j) for i in range(n) for j in range(m) if i or j]
    barrier = pltpu.get_barrier_semaphore()
    for step in steps:
        pl.semaphore_signal(barrier, inc=1, device_id=device(*step), device_id_type=MESH)

    for load in loads[:3]:
        load.wait()
    partial = local_sums(weight, owner, local, n, cells)
    for i in range(n):
        sums[i] = partial[i * types : (i + 1) * types]
    for load in loads[3:]:
        load.wait()
    first = month[0]
    second = lax.rem(first + 1, leaf.shape[0])
    current = mix[0] * leaf[first] + (1.0 - mix[0]) * leaf[second]
    stress = root[:, 0:1] * soil[0:1, :]
    for i in range(1, soil.shape[0]):
        stress += root[:, i : i + 1] * soil[i : i + 1, :]
    effect = (1.0 - jnp.exp(-0.5 * current)) * stress
    own = sums[blk]
    pair[0] = own
    pair[1] = effect

    pl.semaphore_wait(barrier, len(steps))
    for i, j in steps:
        if i:
            source, target, k = (
                sums.at[lax.rem(blk + i, n)],
                got_sums.at[j * (n - 1) + i - 1],
                0,
            )
        else:
            source, target, k = pair, got_pairs.at[j - 1], 1
        pltpu.make_async_remote_copy(
            src_ref=source,
            dst_ref=target,
            send_sem=send_sem.at[k],
            recv_sem=recv_sem.at[k],
            device_id=device(i, j),
            device_id_type=MESH,
        ).start()
    pltpu.make_async_copy(got_sums, got_sums, recv_sem.at[0]).wait()
    pltpu.make_async_copy(got_pairs, got_pairs, recv_sem.at[1]).wait()

    mine, everyone = None, None
    for j in range(m):
        grid = own if j == 0 else got_pairs[j - 1, 0]
        for i in range(n - 1):
            grid = grid + got_sums[j * (n - 1) + i]
        grid = grid * (effect if j == 0 else got_pairs[j - 1, 1])
        if j == 0:
            mine = grid
            everyone = grid
        else:
            everyone = everyone + grid
    out_ref[...] = mine / (1.0 + jnp.sum(everyone, axis=0, keepdims=True))
    pltpu.make_async_copy(got_sums, got_sums, send_sem.at[0]).wait()
    pltpu.make_async_copy(got_pairs, got_pairs, send_sem.at[1]).wait()


def on_device(
    leaf_area, soil_water, root_share, patch_weight, patch_owner, patch_local, month, mix
):
    n, m = lax.axis_size("blk"), lax.axis_size("layer")
    months, types, cells = leaf_area.shape
    patches = patch_local.shape[0]
    owner = patch_owner.reshape(1, patches)
    local = patch_local.reshape(1, patches)
    f32, i32 = jnp.float32, jnp.int32
    return pl.pallas_call(
        functools.partial(kernel, n, m),
        out_shape=pltpu.VMEM((types, cells), f32),
        in_specs=[pl.BlockSpec(memory_space=pl.ANY)] * 8,
        out_specs=pl.BlockSpec(memory_space=pltpu.VMEM),
        scratch_shapes=[
            pltpu.VMEM(leaf_area.shape, f32),
            pltpu.VMEM(soil_water.shape, f32),
            pltpu.VMEM(root_share.shape, f32),
            pltpu.VMEM(patch_weight.shape, f32),
            pltpu.VMEM(owner.shape, i32),
            pltpu.VMEM(local.shape, i32),
            pltpu.SMEM(month.shape, i32),
            pltpu.SMEM(mix.shape, f32),
            pltpu.VMEM((n, types, cells), f32),
            pltpu.VMEM((2, types, cells), f32),
            pltpu.VMEM((m * (n - 1), types, cells), f32),
            pltpu.VMEM((m - 1, 2, types, cells), f32),
            pltpu.SemaphoreType.DMA((8,)),
            pltpu.SemaphoreType.DMA((2,)),
            pltpu.SemaphoreType.DMA((2,)),
        ],
        compiler_params=pltpu.CompilerParams(collective_id=0, has_side_effects=True),
    )(leaf_area, soil_water, root_share, patch_weight, owner, local, month, mix)


def solution(mesh):
    in_specs = (
        P(None, "layer", "blk"),
        P(None, "blk"),
        P("layer", None),
        P("layer", "blk"),
        P("blk", None),
        P("blk"),
        P(),
        P(),
    )
    out_specs = P("layer", "blk")
    return jax.shard_map(
        on_device, mesh=mesh, in_specs=in_specs, out_specs=out_specs, check_vma=False
    )
```

profile of v0, /device:TPU:0, one launch (start us, length us, event | category | flops | bytes accessed | tf_op | source)
XLA Modules:
  0.0 12.0 jit_solution(5810225006042652536)
XLA Ops:
  1.3 10.2 %shard_map.82 = f32[4,128]{1,0:T(4,128)S(1)} custom-call(f32[12,4,128]{2,1,0:T(4,128)} %leaf_hbm.1, f32[10,128]{1,0:T(8,128)} %soil_hbm.1, f32[4,10]{1,0:T(4,128)} %root_hbm.1, f32[4,4096]{1,0:T(4,128)} %weight_hbm.1, s32[1,4096]{1,0:T(1,128)} %bitcast.2, s32[1,4096]{1,0:T(1,128)} %bitcast.3, s32[1]{0:T(128)S(6)} %copy.11.month_hbm, f32[1]{0:T(128)S(6)} %copy.12.mix_hbm), custom_call_target="tpu_custom_call" | custom-call | tf_op jit(solution)/shard_map/pallas_call | solution.py:138
  11.5 0.6 %copy.10 = f32[4,128]{1,0:T(4,128)} copy(f32[4,128]{1,0:T(4,128)S(1)} %shard_map.82) | data formatting | bytes 4096
where the time goes:
time: 12.2 us; the launch traced here: 12 us
  Pallas kernels  10.2 us (84%)
  between operations  1.3 us (11%)
  local copies, waits for them, and re-layouts  0.58 us (5%)
    pallas_call x1, Pallas kernels, on_device(): pl.pallas_call(functools.partial(kernel, n, m), out_shape=pltpu.VMEM((typ...  10.2 us
    unnamed x1, local copies, waits for them, and re-layouts  0.58 us

commit v1 on v0

--- a/solution.py
+++ b/solution.py
@@ -38,13 +38,25 @@
     return total[: owners * types] + total[owners * types :]
 
 
-def kernel(
-    n, m, leaf_hbm, soil_hbm, root_hbm, weight_hbm, owner_hbm, local_hbm, month_hbm, mix_hbm,
-    out_ref, leaf, soil, root, weight, owner, local, month, mix,
-    sums, pair, got_sums, got_pairs, load_sem, send_sem, recv_sem,
+def month_weights(month, mix, out):
+    row = lax.broadcasted_iota(jnp.int32, out.shape, 0)
+    first = month[0]
+    second = lax.rem(first + 1, out.shape[0])
+    blend = jnp.where(row == second, 1.0 - mix[0], 0.0)
+    out[...] = jnp.where(row == first, mix[0], blend)
+
+
+def blank(out):
+    out[...] = jnp.zeros(out.shape, out.dtype)
+
+
+def exchange(
+    n, m, blend, leaf_hbm, soil_hbm, root_hbm, weight_hbm, owner_hbm, local_hbm,
+    sums_out, leaf_out, stress_out, soil, root, weight, owner, local,
+    sums, got_sums, load_sem, send_sem, recv_sem,
 ):
     blk, layer = lax.axis_index("blk"), lax.axis_index("layer")
-    types, cells = out_ref.shape
+    types, cells = sums_out.shape[1:]
     loads = [
         pltpu.make_async_copy(source, target, load_sem.at[i])
         for i, (source, target) in enumerate(
@@ -52,9 +64,7 @@
                 (weight_hbm, weight),
                 (owner_hbm, owner),
                 (local_hbm, local),
-                (month_hbm, month),
-                (mix_hbm, mix),
-                (leaf_hbm, leaf),
+                (leaf_hbm, leaf_out.at[0]),
                 (soil_hbm, soil),
                 (root_hbm, root),
             )
@@ -78,27 +88,15 @@
         sums[i] = partial[i * types : (i + 1) * types]
     for load in loads[3:]:
         load.wait()
-    first = month[0]
-    second = lax.rem(first + 1, leaf.shape[0])
-    current = mix[0] * leaf[first] + (1.0 - mix[0]) * leaf[second]
     stress = root[:, 0:1] * soil[0:1, :]
     for i in range(1, soil.shape[0]):
         stress += root[:, i : i + 1] * soil[i : i + 1, :]
-    effect = (1.0 - jnp.exp(-0.5 * current)) * stress
+    stress_out[0] = stress
     own = sums[blk]
-    pair[0] = own
-    pair[1] = effect
 
     pl.semaphore_wait(barrier, len(steps))
-    for i, j in steps:
-        if i:
-            source, target, k = (
-                sums.at[lax.rem(blk + i, n)],
-                got_sums.at[j * (n - 1) + i - 1],
-                0,
-            )
-        else:
-            source, target, k = pair, got_pairs.at[j - 1], 1
+
+    def send(source, target, k, i, j):
         pltpu.make_async_remote_copy(
             src_ref=source,
             dst_ref=target,
@@ -107,23 +105,46 @@
             device_id=device(i, j),
             device_id_type=MESH,
         ).start()
+
+    for i, j in steps:
+        if i:
+            send(sums.at[lax.rem(blk + i, n)], got_sums.at[j * (n - 1) + i - 1], 0, i, j)
+        else:
+            send(sums.at[blk], got_sums.at[m * (n - 1) + j - 1], 0, i, j)
+    for j in range(1, m):
+        send(stress_out.at[0], stress_out.at[j], 1, 0, j)
+        send(leaf_out.at[0], leaf_out.at[j], 2, 0, j)
     pltpu.make_async_copy(got_sums, got_sums, recv_sem.at[0]).wait()
-    pltpu.make_async_copy(got_pairs, got_pairs, recv_sem.at[1]).wait()
-
-    mine, everyone = None, None
     for j in range(m):
-        grid = own if j == 0 else got_pairs[j - 1, 0]
+        grid = own if j == 0 else got_sums[m * (n - 1) + j - 1]
         for i in range(n - 1):
             grid = grid + got_sums[j * (n - 1) + i]
-        grid = grid * (effect if j == 0 else got_pairs[j - 1, 1])
-        if j == 0:
-            mine = grid
-            everyone = grid
-        else:
-            everyone = everyone + grid
-    out_ref[...] = mine / (1.0 + jnp.sum(everyone, axis=0, keepdims=True))
+        sums_out[j] = grid
+    rest = stress_out.at[pl.ds(1, m - 1)], leaf_out.at[pl.ds(1, m - 1)]
+    for k, ref in enumerate(rest):
+        pltpu.make_async_copy(ref, ref, recv_sem.at[k + 1]).wait()
     pltpu.make_async_copy(got_sums, got_sums, send_sem.at[0]).wait()
-    pltpu.make_async_copy(got_pairs, got_pairs, send_sem.at[1]).wait()
+    for k, ref in enumerate(rest):
+        pltpu.make_async_copy(ref, ref, send_sem.at[k + 1]).wait()
+
+
+def share(current, sums, stress):
+    grid = sums[...] * (1.0 - jnp.exp(-0.5 * current)) * stress[...]
+    return grid[0] / (1.0 + jnp.sum(grid, axis=(0, 1), keepdims=True)[0])
+
+
+def finish_blend(sums, leaf, stress, blend, out):
+    current = blend[0] * leaf[:, 0]
+    for k in range(1, leaf.shape[1]):
+        current += blend[k] * leaf[:, k]
+    out[...] = share(current, sums, stress)
+
+
+def finish_scalars(sums, leaf, stress, month, mix, out):
+    first = month[0]
+    second = lax.rem(first + 1, leaf.shape[1])
+    current = mix[0] * leaf[:, first] + (1.0 - mix[0]) * leaf[:, second]
+    out[...] = share(current, sums, stress)
 
 
 def on_device(
@@ -135,30 +156,53 @@
     owner = patch_owner.reshape(1, patches)
     local = patch_local.reshape(1, patches)
     f32, i32 = jnp.float32, jnp.int32
-    return pl.pallas_call(
-        functools.partial(kernel, n, m),
-        out_shape=pltpu.VMEM((types, cells), f32),
-        in_specs=[pl.BlockSpec(memory_space=pl.ANY)] * 8,
-        out_specs=pl.BlockSpec(memory_space=pltpu.VMEM),
+    hbm = pl.BlockSpec(memory_space=pl.ANY)
+    vmem = pl.BlockSpec(memory_space=pltpu.VMEM)
+    smem = pl.BlockSpec(memory_space=pltpu.SMEM)
+    early = lax.axis_index("blk") * m + lax.axis_index("layer") < 2
+    blend_shape = jax.ShapeDtypeStruct((months, 1, cells), f32)
+
+    def weigh(month, mix):
+        return pl.pallas_call(month_weights, out_shape=blend_shape, in_specs=[smem] * 2, out_specs=vmem)(month, mix)
+
+    def skip(month, mix):
+        return pl.pallas_call(blank, out_shape=blend_shape, out_specs=vmem)()
+
+    blend = lax.cond(early, weigh, skip, month, mix)
+
+    sums, leaf, stress = pl.pallas_call(
+        functools.partial(exchange, n, m),
+        out_shape=[
+            pltpu.VMEM((m, types, cells), f32),
+            pltpu.VMEM((m, months, types, cells), f32),
+            pltpu.VMEM((m, types, cells), f32),
+        ],
+        in_specs=[vmem] + [hbm] * 6,
+        out_specs=[vmem] * 3,
         scratch_shapes=[
-            pltpu.VMEM(leaf_area.shape, f32),
             pltpu.VMEM(soil_water.shape, f32),
             pltpu.VMEM(root_share.shape, f32),
             pltpu.VMEM(patch_weight.shape, f32),
             pltpu.VMEM(owner.shape, i32),
             pltpu.VMEM(local.shape, i32),
-            pltpu.SMEM(month.shape, i32),
-            pltpu.SMEM(mix.shape, f32),
             pltpu.VMEM((n, types, cells), f32),
-            pltpu.VMEM((2, types, cells), f32),
-            pltpu.VMEM((m * (n - 1), types, cells), f32),
-            pltpu.VMEM((m - 1, 2, types, cells), f32),
-            pltpu.SemaphoreType.DMA((8,)),
-            pltpu.SemaphoreType.DMA((2,)),
-            pltpu.SemaphoreType.DMA((2,)),
+            pltpu.VMEM((m * (n - 1) + m - 1, types, cells), f32),
+            pltpu.SemaphoreType.DMA((6,)),
+            pltpu.SemaphoreType.DMA((3,)),
+            pltpu.SemaphoreType.DMA((3,)),
         ],
         compiler_params=pltpu.CompilerParams(collective_id=0, has_side_effects=True),
-    )(leaf_area, soil_water, root_share, patch_weight, owner, local, month, mix)
+    )(blend, leaf_area, soil_water, root_share, patch_weight, owner, local)
+
+    out_shape = jax.ShapeDtypeStruct((types, cells), f32)
+
+    def early_finish(sums, leaf, stress, blend, month, mix):
+        return pl.pallas_call(finish_blend, out_shape=out_shape, in_specs=[vmem] * 4, out_specs=vmem)(sums, leaf, stress, blend)
+
+    def late_finish(sums, leaf, stress, blend, month, mix):
+        return pl.pallas_call(finish_scalars, out_shape=out_shape, in_specs=[vmem] * 3 + [smem] * 2, out_specs=vmem)(sums, leaf, stress, month, mix)
+
+    return lax.cond(early, early_finish, late_finish, sums, leaf, stress, blend, month, mix)
 
 
 def solution(mesh):

time: 12.2 us -> 11.1 us (0.910)
  the two profiles are of different devices: /device:TPU:0 before, /device:TPU:3 now
where the time goes in v1:
time: 11.1 us; the launch traced here: 10.9 us
  Pallas kernels  10.3 us (93%)
  local copies, waits for them, and re-layouts  0.57 us (5%)
    pallas_call x1, Pallas kernels, on_device(): pl.pallas_call(functools.partial(exchange, n, m), out_shape=[pltpu.VMEM((...  8.99 us
    pallas_call x1, Pallas kernels, late_finish(): pl.pallas_call(finish_scalars, out_shape=out_shape, in_specs=[vmem] * 3 +...  1.33 us
    unnamed x2, local copies, waits for them, and re-layouts  0.57 us

profile of v1, /device:TPU:3, one launch (start us, length us, event | category | flops | bytes accessed | tf_op | source)
XLA Modules:
  0.0 10.9 jit_solution(16866352670343020041)
XLA Ops:
  0.0 9.0 %shard_map.84 = (f32[4,4,128]{2,1,0:T(4,128)S(1)}, f32[4,12,4,128]{3,2,1,0:T(4,128)S(1)}, f32[4,4,128]{2,1,0:T(4,128)S(1)}) custom-call(f32[12,1,128]{2,1,0:T(1,128)S(1)} %get-tuple-element.53.blend, f32[12,4,128]{2,1,0:T(4,128)} %leaf_hbm.1, f32[10,128]{1,0:T(8,128)} %soil_hbm.1, f32[4,10]{1,0:T(4,128)} %root_hbm.1, f32[4,4096]{1,0:T(4,128)} %weight_hbm.1, ...), custom_call_target="tpu_custom_call" | custom-call | tf_op jit(solution)/shard_map/pallas_call | solution.py:173
  9.0 1.3 %conditional.3 = (f32[4,128]{1,0:T(4,128)S(1)}) conditional(s32[]{:T(128)} %convert_element_type.4, (f32[4,4,128]{2,1,0:T(4,128)S(1)}, f32[4,12,4,128]{3,2,1,0:T(4,128)S(1)}, f32[4,4,128]{2,1,0:T(4,128)S(1)}, s32[1]{0:T(128)}, f32[1]{0:T(128)}) %tuple.19, (f32[4,4,128]{2,1,0:T(4,128)S(1)}, f32[4,12,4,128]{3,2,1,0:T(4,128)S(1)}, ...), branch_computations={%region_2.0_spmd, %region_3.0_spmd} | conditional | bytes 8 | solution.py:205
  9.0 1.3 %branch_0_fun.3 = f32[4,128]{1,0:T(4,128)S(1)} custom-call(f32[4,4,128]{2,1,0:T(4,128)S(1)} %get-tuple-element.35.sums, f32[4,12,4,128]{3,2,1,0:T(4,128)S(1)} %get-tuple-element.36.leaf, f32[4,4,128]{2,1,0:T(4,128)S(1)} %get-tuple-element.37.stress, s32[1]{0:T(128)} %get-tuple-element.38.month, f32[1]{0:T(128)} %get-tuple-element.39.mix), custom_call_target="tpu_custom_call" | custom-call | tf_op jit(solution)/shard_map/cond/branch_0_fun/pallas_call | solution.py:203
  10.4 0.0 copy-start
  10.4 0.6 %copy-done = f32[4,128]{1,0:T(4,128)} copy-done((f32[4,128]{1,0:T(4,128)}, f32[4,128]{1,0:T(4,128)S(1)}, u32[]{:S(2)}) %copy-start) | copy-done | bytes 2072
  (2 shorter events, 0.0 us)
Async XLA Ops:
  10.4 0.6 %copy-start = (f32[4,128]{1,0:T(4,128)}, f32[4,128]{1,0:T(4,128)S(1)}, u32[]{:S(2)}) copy-start(f32[4,128]{1,0:T(4,128)S(1)} %get-tuple-element.54) | copy-start | bytes 6148

commit v2 on v0

v2 whole, which is shorter than its diff:
```python
import functools

import jax
import jax.numpy as jnp
from jax import lax
from jax.experimental import pallas as pl
from jax.experimental.pallas import tpu as pltpu
from jax.sharding import PartitionSpec as P

MESH = pl.DeviceIdType.MESH
CHUNK = 512
NEAR = 2


def local_sums(weight, owner, local, owners, cells):
    types, patches = weight.shape
    chunk = CHUNK if patches % CHUNK == 0 else patches
    tall = 16
    rows = lax.broadcasted_iota(jnp.int32, (tall, chunk), 0) // types
    groups = owners * types // tall
    per = tall // types
    row_owner = [(rows + per * g).astype(jnp.int16) for g in range(groups)]
    cell = lax.broadcasted_iota(jnp.int32, (cells, chunk), 0).astype(jnp.int16)
    zero, one = jnp.bfloat16(0.0), jnp.bfloat16(1.0)
    total = None
    for start in range(0, patches, chunk):
        part = slice(start, start + chunk)
        w = weight[:, part]
        w = jnp.concatenate([w] * (8 // types), axis=0)
        high = w.astype(jnp.bfloat16).astype(jnp.float32)
        low = w - high
        high, low = [
            jnp.concatenate([piece] * (tall // 8), axis=0).astype(jnp.bfloat16)
            for piece in (high, low)
        ]
        who = jnp.broadcast_to(owner[:, part], (tall, chunk)).astype(jnp.int16)
        named = [row == who for row in row_owner]
        left = jnp.concatenate(
            [jnp.where(name, piece, zero) for piece in (high, low) for name in named], axis=0
        )
        where = jnp.broadcast_to(local[:, part], (tall, chunk)).astype(jnp.int16)
        where = jnp.concatenate([where] * (cells // tall), axis=0)
        table = jnp.where(cell == where, one, zero).astype(jnp.float8_e4m3fn)
        product = lax.dot_general(
            left, table, (((1,), (1,)), ((), ())), preferred_element_type=jnp.float32
        )
        total = product if total is None else total + product
    return total[: owners * types] + total[owners * types :]


def spread(value, out):
    out[...] = jnp.zeros(out.shape, out.dtype) + value[0].astype(out.dtype)


def blank(out):
    out[...] = jnp.zeros(out.shape, out.dtype)


def kernel(
    n, m, given, leaf_hbm, soil_hbm, root_hbm, weight_hbm, owner_hbm, local_hbm,
    out_ref, soil, root, weight, owner, local, leaf, scalars, sums, pairs, got,
    load_sem, send_sem, recv_sem, met_sem,
):
    blk, layer = lax.axis_index("blk"), lax.axis_index("layer")
    types, cells = out_ref.shape
    months = leaf.shape[1]
    everywhere = [(b, k) for b in range(n) for k in range(m)]
    is_near = jnp.logical_and(blk == 0, layer >= NEAR)
    pair_sem, leaf_sem, scalar_sem = n, n + 1, n + 2
    loads = [
        pltpu.make_async_copy(source, target, load_sem.at[i])
        for i, (source, target) in enumerate(
            (
                (weight_hbm, weight),
                (owner_hbm, owner),
                (local_hbm, local),
                (soil_hbm, soil),
                (root_hbm, root),
                (leaf_hbm, leaf.at[layer]),
            )
        )
    ]
    for load in loads:
        load.start()

    barrier = pltpu.get_barrier_semaphore()

    def greet(semaphore, b, k):
        pl.semaphore_signal(semaphore, inc=1, device_id=(b, k), device_id_type=MESH)

    peers = [lax.rem(layer + j, m) for j in range(1, m)]
    for k in peers:
        greet(barrier, blk, k)
    for b in range(n):

        @pl.when(blk != b)
        def _():
            for k in range(m if b else min(NEAR, m)):
                greet(barrier, b, k)

    for load in loads[:3]:
        load.wait()
    partial = local_sums(weight, owner, local, n, cells)
    for i in range(n):
        sums[i] = partial[i * types : (i + 1) * types]
    for load in loads[3:]:
        load.wait()
    stress = root[:, 0:1] * soil[0:1, :]
    for i in range(1, soil.shape[0]):
        stress += root[:, i : i + 1] * soil[i : i + 1, :]
    pairs[layer, 0] = sums[blk]
    pairs[layer, 1] = stress
    got[blk] = jnp.zeros(got.shape[1:], got.dtype)

    def send(source, target, sem, b, k):
        pltpu.make_async_remote_copy(
            src_ref=source,
            dst_ref=target,
            send_sem=send_sem.at[sem],
            recv_sem=recv_sem.at[sem],
            device_id=(b, k),
            device_id_type=MESH,
        ).start()

    def send_peers():
        for k in peers:
            send(pairs.at[layer], pairs.at[layer], pair_sem, blk, k)
        for k in peers:
            send(leaf.at[layer], leaf.at[layer], leaf_sem, blk, k)

    pl.semaphore_wait(barrier, jnp.where(is_near, m - 1, n * m - 1))

    @pl.when(is_near)
    def _():
        send_peers()
        pl.semaphore_wait(met_sem, (n - 1) * m)

    for b in range(n):

        @pl.when(blk != b)
        def _():
            for k in range(m):
                send(sums.at[b], got.at[blk, layer], blk, b, k)
            if b == 0:
                for k in range(NEAR, m):
                    greet(met_sem, 0, k)

    pl.when(jnp.logical_not(is_near))(send_peers)

    reads = [jnp.logical_and(blk == 0, layer == k) for k in range(2)]
    for k, read in enumerate(reads):
        row = scalars.at[k]

        @pl.when(read)
        def _():
            for place in everywhere:
                if place != (0, k):
                    send(given, row, scalar_sem + k, *place)
            row[...] = given[...]

        @pl.when(jnp.logical_not(read))
        def _():
            pltpu.make_async_copy(row, row, recv_sem.at[scalar_sem + k]).wait()

    others = pl.ds(0, m - 1)
    arrivals = [(pairs.at[others], pair_sem), (leaf.at[others], leaf_sem)]
    for ref, sem in arrivals:
        pltpu.make_async_copy(ref, ref, recv_sem.at[sem]).wait()
    first, mix = scalars[0], scalars[1]
    second = jnp.where(first == months - 1, 0.0, first + 1.0)
    share = [
        jnp.where(first == k, mix, jnp.where(second == k, 1.0 - mix, 0.0)) for k in range(months)
    ]
    effects, grids = [], []
    for k in range(m):
        current = share[0] * leaf[k, 0]
        for i in range(1, months):
            current += share[i] * leaf[k, i]
        effects.append((1.0 - jnp.exp(-0.5 * current)) * pairs[k, 1])
        grids.append(pairs[k, 0])
    for b in range(n):

        @pl.when(blk != b)
        def _():
            pltpu.make_async_copy(got.at[b], got.at[b], recv_sem.at[b]).wait()

        grids = [grid + got[b, k] for k, grid in enumerate(grids)]
    mine, everyone = None, None
    for k in range(m):
        grid = grids[k] * effects[k]
        mine = grid if k == 0 else jnp.where(layer == k, grid, mine)
        everyone = grid if k == 0 else everyone + grid
    out_ref[...] = mine / (1.0 + jnp.sum(everyone, axis=0, keepdims=True))

    sent = got.at[pl.ds(0, n - 1)]
    pltpu.make_async_copy(sent, sent, send_sem.at[blk]).wait()
    for ref, sem in arrivals:
        pltpu.make_async_copy(ref, ref, send_sem.at[sem]).wait()
    for k, read in enumerate(reads):
        row = scalars.at[k]

        @pl.when(read)
        def _():
            for _ in everywhere[1:]:
                pltpu.make_async_copy(row, row, send_sem.at[scalar_sem + k]).wait()


def on_device(
    leaf_area, soil_water, root_share, patch_weight, patch_owner, patch_local, month, mix
):
    n, m = lax.axis_size("blk"), lax.axis_size("layer")
    months, types, cells = leaf_area.shape
    patches = patch_local.shape[0]
    owner = patch_owner.reshape(1, patches)
    local = patch_local.reshape(1, patches)
    f32, i32 = jnp.float32, jnp.int32
    hbm = pl.BlockSpec(memory_space=pl.ANY)
    vmem = pl.BlockSpec(memory_space=pltpu.VMEM)
    smem = pl.BlockSpec(memory_space=pltpu.SMEM)
    row = jax.ShapeDtypeStruct((1, cells), f32)

    def reader(value):
        return pl.pallas_call(spread, out_shape=row, in_specs=[smem], out_specs=vmem)(value)

    role = jnp.where(lax.axis_index("blk") == 0, jnp.minimum(lax.axis_index("layer"), 2), 2)
    given = lax.switch(
        role,
        [
            lambda month, mix: reader(month),
            lambda month, mix: reader(mix),
            lambda month, mix: pl.pallas_call(blank, out_shape=row, out_specs=vmem)(),
        ],
        month,
        mix,
    )
    return pl.pallas_call(
        functools.partial(kernel, n, m),
        out_shape=pltpu.VMEM((types, cells), f32),
        in_specs=[vmem] + [hbm] * 6,
        out_specs=vmem,
        scratch_shapes=[
            pltpu.VMEM(soil_water.shape, f32),
            pltpu.VMEM(root_share.shape, f32),
            pltpu.VMEM(patch_weight.shape, f32),
            pltpu.VMEM(owner.shape, i32),
            pltpu.VMEM(local.shape, i32),
            pltpu.VMEM((m, months, types, cells), f32),
            pltpu.VMEM((2, *row.shape), f32),
            pltpu.VMEM((n, types, cells), f32),
            pltpu.VMEM((m, 2, types, cells), f32),
            pltpu.VMEM((n, m, types, cells), f32),
            pltpu.SemaphoreType.DMA((6,)),
            pltpu.SemaphoreType.DMA((n + 4,)),
            pltpu.SemaphoreType.DMA((n + 4,)),
            pltpu.SemaphoreType.REGULAR,
        ],
        compiler_params=pltpu.CompilerParams(collective_id=0, has_side_effects=True),
    )(given, leaf_area, soil_water, root_share, patch_weight, owner, local)


def solution(mesh):
    in_specs = (
        P(None, "layer", "blk"),
        P(None, "blk"),
        P("layer", None),
        P("layer", "blk"),
        P("blk", None),
        P("blk"),
        P(),
        P(),
    )
    out_specs = P("layer", "blk")
    return jax.shard_map(
        on_device, mesh=mesh, in_specs=in_specs, out_specs=out_specs, check_vma=False
    )
```

time: 12.2 us -> 10.8 us (0.89)
  between operations: 1.3 us -> 0.02 us
  Pallas kernels: 10.2 us -> 10 us
    pallas_call x1, Pallas kernels: 10.2 us -> 9.39 us  [on_device(): pl.pallas_call(functools.partial(kernel, n, m), out_shape=pltpu.VMEM((typ...]
    pallas_call x0 -> x1, Pallas kernels: none -> 0.65 us  [reader(): pl.pallas_call(spread, out_shape=row, in_specs=[smem], out_specs=vmem)]
where the time goes in v2:
time: 10.8 us; the launch traced here: 10.6 us
  Pallas kernels  10 us (93%)
  local copies, waits for them, and re-layouts  0.58 us (5%)
    pallas_call x1, Pallas kernels, on_device(): pl.pallas_call(functools.partial(kernel, n, m), out_shape=pltpu.VMEM((typ...  9.39 us
    pallas_call x1, Pallas kernels, reader(): pl.pallas_call(spread, out_shape=row, in_specs=[smem], out_specs=vmem)  0.65 us
    unnamed x1, local copies, waits for them, and re-layouts  0.58 us

profile of v2, /device:TPU:0, one launch (start us, length us, event | category | flops | bytes accessed | tf_op | source)
XLA Modules:
  0.0 10.6 jit_solution(4338382946241363161)
XLA Ops:
  0.0 0.7 %conditional.1 = (f32[1,128]{1,0:T(1,128)S(1)}) conditional(s32[]{:T(128)} %clamp.3, (s32[1]{0:T(128)}) %tuple.15, (f32[1]{0:T(128)}) %tuple.16, () %tuple.14), branch_computations={%region_0.1_spmd, %region_1.2_spmd, %region_2.3_spmd} | conditional | bytes 8 | solution.py:226
  0.0 0.6 %branch_0_fun.1 = f32[1,128]{1,0:T(1,128)S(1)} custom-call(s32[1]{0:T(128)} %get-tuple-element.12.value), custom_call_target="tpu_custom_call" | custom-call | tf_op jit(solution)/shard_map/cond/branch_0_fun/pallas_call | solution.py:223
  0.7 9.4 %shard_map.90 = f32[4,128]{1,0:T(4,128)S(1)} custom-call(f32[1,128]{1,0:T(1,128)S(1)} %get-tuple-element.15.given, f32[12,4,128]{2,1,0:T(4,128)} %leaf_hbm.1, f32[10,128]{1,0:T(8,128)} %soil_hbm.1, f32[4,10]{1,0:T(4,128)} %root_hbm.1, f32[4,4096]{1,0:T(4,128)} %weight_hbm.1, s32[1,4096]{1,0:T(1,128)} %bitcast.2, s32[1,4096]{1,0:T(1,128)} %bitcast.3), custom_call_target="tpu_custom_call" | custom-call | tf_op jit(solution)/shard_map/pallas_call | solution.py:236
  10.1 0.6 %copy.15 = f32[4,128]{1,0:T(4,128)} copy(f32[4,128]{1,0:T(4,128)S(1)} %shard_map.90) | data formatting | bytes 4096

commit v3 on v2

--- a/solution.py
+++ b/solution.py
@@ -67,18 +67,17 @@
     everywhere = [(b, k) for b in range(n) for k in range(m)]
     is_near = jnp.logical_and(blk == 0, layer >= NEAR)
     pair_sem, leaf_sem, scalar_sem = n, n + 1, n + 2
+    copies = [
+        (weight_hbm, weight),
+        (owner_hbm, owner),
+        (local_hbm, local),
+        (root_hbm, root),
+        (soil_hbm, soil),
+        (leaf_hbm, leaf.at[layer]),
+    ]
     loads = [
         pltpu.make_async_copy(source, target, load_sem.at[i])
-        for i, (source, target) in enumerate(
-            (
-                (weight_hbm, weight),
-                (owner_hbm, owner),
-                (local_hbm, local),
-                (soil_hbm, soil),
-                (root_hbm, root),
-                (leaf_hbm, leaf.at[layer]),
-            )
-        )
+        for i, (source, target) in enumerate(copies)
     ]
     for load in loads:
         load.start()
@@ -98,19 +97,18 @@
             for k in range(m if b else min(NEAR, m)):
                 greet(barrier, b, k)
 
+    got[blk] = jnp.zeros(got.shape[1:], got.dtype)
+    for load in loads[3:5]:
+        load.wait()
+    stress = root[:, 0:1] * soil[0:1, :]
+    for i in range(1, soil.shape[0]):
+        stress += root[:, i : i + 1] * soil[i : i + 1, :]
+    pairs[layer, 1] = stress
     for load in loads[:3]:
         load.wait()
     partial = local_sums(weight, owner, local, n, cells)
     for i in range(n):
         sums[i] = partial[i * types : (i + 1) * types]
-    for load in loads[3:]:
-        load.wait()
-    stress = root[:, 0:1] * soil[0:1, :]
-    for i in range(1, soil.shape[0]):
-        stress += root[:, i : i + 1] * soil[i : i + 1, :]
-    pairs[layer, 0] = sums[blk]
-    pairs[layer, 1] = stress
-    got[blk] = jnp.zeros(got.shape[1:], got.dtype)
 
     def send(source, target, sem, b, k):
         pltpu.make_async_remote_copy(
@@ -132,6 +130,8 @@
 
     @pl.when(is_near)
     def _():
+        pairs[layer, 0] = sums[blk]
+        loads[5].wait()
         send_peers()
         pl.semaphore_wait(met_sem, (n - 1) * m)
 
@@ -141,11 +141,14 @@
         def _():
             for k in range(m):
                 send(sums.at[b], got.at[blk, layer], blk, b, k)
-            if b == 0:
-                for k in range(NEAR, m):
-                    greet(met_sem, 0, k)
-
-    pl.when(jnp.logical_not(is_near))(send_peers)
+                if b == 0 and k >= NEAR:
+                    greet(met_sem, b, k)
+
+    @pl.when(jnp.logical_not(is_near))
+    def _():
+        pairs[layer, 0] = sums[blk]
+        loads[5].wait()
+        send_peers()
 
     reads = [jnp.logical_and(blk == 0, layer == k) for k in range(2)]
     for k, read in enumerate(reads):
@@ -179,6 +182,18 @@
         effects.append((1.0 - jnp.exp(-0.5 * current)) * pairs[k, 1])
         grids.append(pairs[k, 0])
     for b in range(n):
+        if b == n - 1:
+            sent = got.at[pl.ds(0, n - 1)]
+            pltpu.make_async_copy(sent, sent, send_sem.at[blk]).wait()
+            for ref, sem in arrivals:
+                pltpu.make_async_copy(ref, ref, send_sem.at[sem]).wait()
+            for k, read in enumerate(reads):
+                row = scalars.at[k]
+
+                @pl.when(read)
+                def _():
+                    for _ in everywhere[1:]:
+                        pltpu.make_async_copy(row, row, send_sem.at[scalar_sem + k]).wait()
 
         @pl.when(blk != b)
         def _():
@@ -191,18 +206,6 @@
         mine = grid if k == 0 else jnp.where(layer == k, grid, mine)
         everyone = grid if k == 0 else everyone + grid
     out_ref[...] = mine / (1.0 + jnp.sum(everyone, axis=0, keepdims=True))
-
-    sent = got.at[pl.ds(0, n - 1)]
-    pltpu.make_async_copy(sent, sent, send_sem.at[blk]).wait()
-    for ref, sem in arrivals:
-        pltpu.make_async_copy(ref, ref, send_sem.at[sem]).wait()
-    for k, read in enumerate(reads):
-        row = scalars.at[k]
-
-        @pl.when(read)
-        def _():
-            for _ in everywhere[1:]:
-                pltpu.make_async_copy(row, row, send_sem.at[scalar_sem + k]).wait()
 
 
 def on_device(

time: 10.8 us -> 10.7 us (level)
  no operation moved by 1% of the time
where the time goes in v3:
time: 10.7 us; the launch traced here: 10.6 us
  Pallas kernels  9.96 us (93%)
  local copies, waits for them, and re-layouts  0.58 us (5%)
    pallas_call x1, Pallas kernels, on_device(): pl.pallas_call(functools.partial(kernel, n, m), out_shape=pltpu.VMEM((typ...  9.31 us
    pallas_call x1, Pallas kernels, reader(): pl.pallas_call(spread, out_shape=row, in_specs=[smem], out_specs=vmem)  0.65 us
    unnamed x1, local copies, waits for them, and re-layouts  0.58 us

profile of v3, /device:TPU:0, one launch (start us, length us, event | category | flops | bytes accessed | tf_op | source)
XLA Modules:
  0.0 10.6 jit_solution(6468187014074624622)
XLA Ops:
  0.0 0.7 %conditional.1 = (f32[1,128]{1,0:T(1,128)S(1)}) conditional(s32[]{:T(128)} %clamp.3, (s32[1]{0:T(128)}) %tuple.15, (f32[1]{0:T(128)}) %tuple.16, () %tuple.14), branch_computations={%region_0.1_spmd, %region_1.2_spmd, %region_2.3_spmd} | conditional | bytes 8 | solution.py:229
  0.0 0.6 %branch_0_fun.1 = f32[1,128]{1,0:T(1,128)S(1)} custom-call(s32[1]{0:T(128)} %get-tuple-element.12.value), custom_call_target="tpu_custom_call" | custom-call | tf_op jit(solution)/shard_map/cond/branch_0_fun/pallas_call | solution.py:226
  0.7 9.3 %shard_map.90 = f32[4,128]{1,0:T(4,128)S(1)} custom-call(f32[1,128]{1,0:T(1,128)S(1)} %get-tuple-element.15.given, f32[12,4,128]{2,1,0:T(4,128)} %leaf_hbm.1, f32[10,128]{1,0:T(8,128)} %soil_hbm.1, f32[4,10]{1,0:T(4,128)} %root_hbm.1, f32[4,4096]{1,0:T(4,128)} %weight_hbm.1, s32[1,4096]{1,0:T(1,128)} %bitcast.2, s32[1,4096]{1,0:T(1,128)} %bitcast.3), custom_call_target="tpu_custom_call" | custom-call | tf_op jit(solution)/shard_map/pallas_call | solution.py:239
  10.0 0.6 %copy.15 = f32[4,128]{1,0:T(4,128)} copy(f32[4,128]{1,0:T(4,128)S(1)} %shard_map.90) | data formatting | bytes 4096

commit v4 on v3

--- a/solution.py
+++ b/solution.py
@@ -56,31 +56,37 @@
     out[...] = jnp.zeros(out.shape, out.dtype)
 
 
+def put_rows(share, out, sem):
+    for i in range(share.shape[0]):
+        row = pl.ds(i, 1)
+        pltpu.make_async_copy(share.at[row], out.at[row], sem).start()
+    pltpu.make_async_copy(share, out, sem).wait()
+
+
 def kernel(
     n, m, given, leaf_hbm, soil_hbm, root_hbm, weight_hbm, owner_hbm, local_hbm,
     out_ref, soil, root, weight, owner, local, leaf, scalars, sums, pairs, got,
-    load_sem, send_sem, recv_sem, met_sem,
+    tally, load_sem, side_sem, root_sem, send_sem, sum_sem, part_sem, met_sem,
 ):
     blk, layer = lax.axis_index("blk"), lax.axis_index("layer")
     types, cells = out_ref.shape
     months = leaf.shape[1]
     everywhere = [(b, k) for b in range(n) for k in range(m)]
     is_near = jnp.logical_and(blk == 0, layer >= NEAR)
-    pair_sem, leaf_sem, scalar_sem = n, n + 1, n + 2
-    copies = [
-        (weight_hbm, weight),
-        (owner_hbm, owner),
-        (local_hbm, local),
-        (root_hbm, root),
-        (soil_hbm, soil),
-        (leaf_hbm, leaf.at[layer]),
-    ]
-    loads = [
-        pltpu.make_async_copy(source, target, load_sem.at[i])
-        for i, (source, target) in enumerate(copies)
-    ]
-    for load in loads:
-        load.start()
+    parts = (m - 1) * (2 + months) * types
+
+    def settle(semaphore, rows):
+        pltpu.make_async_copy(tally.at[pl.ds(0, rows)], tally.at[pl.ds(0, rows)], semaphore).wait()
+
+    for source, target, semaphore in (
+        (weight_hbm, weight, load_sem),
+        (owner_hbm, owner, load_sem),
+        (local_hbm, local, load_sem),
+        (root_hbm, root, root_sem),
+        (soil_hbm, soil, side_sem),
+        (leaf_hbm, leaf.at[layer], side_sem),
+    ):
+        pltpu.make_async_copy(source, target, semaphore).start()
 
     barrier = pltpu.get_barrier_semaphore()
 
@@ -98,14 +104,7 @@
                 greet(barrier, b, k)
 
     got[blk] = jnp.zeros(got.shape[1:], got.dtype)
-    for load in loads[3:5]:
-        load.wait()
-    stress = root[:, 0:1] * soil[0:1, :]
-    for i in range(1, soil.shape[0]):
-        stress += root[:, i : i + 1] * soil[i : i + 1, :]
-    pairs[layer, 1] = stress
-    for load in loads[:3]:
-        load.wait()
+    settle(load_sem, (types + 2) * weight.shape[1] // cells)
     partial = local_sums(weight, owner, local, n, cells)
     for i in range(n):
         sums[i] = partial[i * types : (i + 1) * types]
@@ -114,24 +113,29 @@
         pltpu.make_async_remote_copy(
             src_ref=source,
             dst_ref=target,
-            send_sem=send_sem.at[sem],
-            recv_sem=recv_sem.at[sem],
+            send_sem=send_sem,
+            recv_sem=sem,
             device_id=(b, k),
             device_id_type=MESH,
         ).start()
 
     def send_peers():
+        pltpu.make_async_copy(root_hbm, root, root_sem).wait()
+        settle(side_sem, soil.shape[0] + months * types)
+        stress = root[:, 0:1] * soil[0:1, :]
+        for i in range(1, soil.shape[0]):
+            stress += root[:, i : i + 1] * soil[i : i + 1, :]
+        pairs[layer, 0] = sums[blk]
+        pairs[layer, 1] = stress
         for k in peers:
-            send(pairs.at[layer], pairs.at[layer], pair_sem, blk, k)
+            send(pairs.at[layer], pairs.at[layer], part_sem, blk, k)
         for k in peers:
-            send(leaf.at[layer], leaf.at[layer], leaf_sem, blk, k)
+            send(leaf.at[layer], leaf.at[layer], part_sem, blk, k)
 
     pl.semaphore_wait(barrier, jnp.where(is_near, m - 1, n * m - 1))
 
     @pl.when(is_near)
     def _():
-        pairs[layer, 0] = sums[blk]
-        loads[5].wait()
         send_peers()
         pl.semaphore_wait(met_sem, (n - 1) * m)
 
@@ -140,14 +144,12 @@
         @pl.when(blk != b)
         def _():
             for k in range(m):
-                send(sums.at[b], got.at[blk, layer], blk, b, k)
+                send(sums.at[b], got.at[blk, layer], sum_sem, b, k)
                 if b == 0 and k >= NEAR:
                     greet(met_sem, b, k)
 
     @pl.when(jnp.logical_not(is_near))
     def _():
-        pairs[layer, 0] = sums[blk]
-        loads[5].wait()
         send_peers()
 
     reads = [jnp.logical_and(blk == 0, layer == k) for k in range(2)]
@@ -158,17 +160,12 @@
         def _():
             for place in everywhere:
                 if place != (0, k):
-                    send(given, row, scalar_sem + k, *place)
+                    send(given, row, part_sem, *place)
             row[...] = given[...]
 
-        @pl.when(jnp.logical_not(read))
-        def _():
-            pltpu.make_async_copy(row, row, recv_sem.at[scalar_sem + k]).wait()
-
-    others = pl.ds(0, m - 1)
-    arrivals = [(pairs.at[others], pair_sem), (leaf.at[others], leaf_sem)]
-    for ref, sem in arrivals:
-        pltpu.make_async_copy(ref, ref, recv_sem.at[sem]).wait()
+    is_reader = jnp.logical_or(*reads)
+    pl.when(is_reader)(lambda: settle(part_sem, parts + 1))
+    pl.when(jnp.logical_not(is_reader))(lambda: settle(part_sem, parts + 2))
     first, mix = scalars[0], scalars[1]
     second = jnp.where(first == months - 1, 0.0, first + 1.0)
     share = [
@@ -181,24 +178,11 @@
             current += share[i] * leaf[k, i]
         effects.append((1.0 - jnp.exp(-0.5 * current)) * pairs[k, 1])
         grids.append(pairs[k, 0])
+    sent = (n - 1) * m * types + parts
+    pl.when(is_reader)(lambda: settle(send_sem, sent + n * m - 1))
+    pl.when(jnp.logical_not(is_reader))(lambda: settle(send_sem, sent))
+    settle(sum_sem, (n - 1) * m * types)
     for b in range(n):
-        if b == n - 1:
-            sent = got.at[pl.ds(0, n - 1)]
-            pltpu.make_async_copy(sent, sent, send_sem.at[blk]).wait()
-            for ref, sem in arrivals:
-                pltpu.make_async_copy(ref, ref, send_sem.at[sem]).wait()
-            for k, read in enumerate(reads):
-                row = scalars.at[k]
-
-                @pl.when(read)
-                def _():
-                    for _ in everywhere[1:]:
-                        pltpu.make_async_copy(row, row, send_sem.at[scalar_sem + k]).wait()
-
-        @pl.when(blk != b)
-        def _():
-            pltpu.make_async_copy(got.at[b], got.at[b], recv_sem.at[b]).wait()
-
         grids = [grid + got[b, k] for k, grid in enumerate(grids)]
     mine, everyone = None, None
     for k in range(m):
@@ -221,6 +205,11 @@
     vmem = pl.BlockSpec(memory_space=pltpu.VMEM)
     smem = pl.BlockSpec(memory_space=pltpu.SMEM)
     row = jax.ShapeDtypeStruct((1, cells), f32)
+    rows = max(
+        (types + 2) * patches // cells,
+        (n - 1) * m * types + (m - 1) * (2 + months) * types + n * m,
+        soil_water.shape[0] + months * types,
+    )
 
     def reader(value):
         return pl.pallas_call(spread, out_shape=row, in_specs=[smem], out_specs=vmem)(value)
@@ -236,7 +225,7 @@
         month,
         mix,
     )
-    return pl.pallas_call(
+    share = pl.pallas_call(
         functools.partial(kernel, n, m),
         out_shape=pltpu.VMEM((types, cells), f32),
         in_specs=[vmem] + [hbm] * 6,
@@ -252,13 +241,19 @@
             pltpu.VMEM((n, types, cells), f32),
             pltpu.VMEM((m, 2, types, cells), f32),
             pltpu.VMEM((n, m, types, cells), f32),
-            pltpu.SemaphoreType.DMA((6,)),
-            pltpu.SemaphoreType.DMA((n + 4,)),
-            pltpu.SemaphoreType.DMA((n + 4,)),
+            pltpu.VMEM((rows, cells), f32),
+            *[pltpu.SemaphoreType.DMA] * 6,
             pltpu.SemaphoreType.REGULAR,
         ],
         compiler_params=pltpu.CompilerParams(collective_id=0, has_side_effects=True),
     )(given, leaf_area, soil_water, root_share, patch_weight, owner, local)
+    return pl.pallas_call(
+        put_rows,
+        out_shape=jax.ShapeDtypeStruct(share.shape, f32),
+        in_specs=[vmem],
+        out_specs=hbm,
+        scratch_shapes=[pltpu.SemaphoreType.DMA],
+    )(pltpu.with_memory_space_constraint(share, pltpu.VMEM))
 
 
 def solution(mesh):

time: 10.7 us -> 10.5 us (0.981)
  local copies, waits for them, and re-layouts: 0.58 us -> 0 us
  Pallas kernels: 9.96 us -> 10.3 us
    unnamed x1 -> x0, local copies, waits for them, and re-layouts: 0.58 us -> none
    pallas_call x0 -> x1, Pallas kernels: none -> 0.53 us  [on_device(): pl.pallas_call(put_rows, out_shape=jax.ShapeDtypeStruct(share.shape, f32)...]
    pallas_call x1, Pallas kernels: 9.31 us -> 9.09 us  [on_device(): pl.pallas_call(functools.partial(kernel, n, m), out_shape=pltpu.VMEM((typ...]
where the time goes in v4:
time: 10.5 us; the launch traced here: 10.3 us
  Pallas kernels  10.3 us (98%)
    pallas_call x1, Pallas kernels, on_device(): pl.pallas_call(functools.partial(kernel, n, m), out_shape=pltpu.VMEM((typ...  9.09 us
    pallas_call x1, Pallas kernels, reader(): pl.pallas_call(spread, out_shape=row, in_specs=[smem], out_specs=vmem)  0.65 us
    pallas_call x1, Pallas kernels, on_device(): pl.pallas_call(put_rows, out_shape=jax.ShapeDtypeStruct(share.shape, f32)...  0.53 us

profile of v4, /device:TPU:0, one launch (start us, length us, event | category | flops | bytes accessed | tf_op | source)
XLA Modules:
  0.0 10.3 jit_solution(7787268578318481342)
XLA Ops:
  0.0 0.7 %conditional.1 = (f32[1,128]{1,0:T(1,128)S(1)}) conditional(s32[]{:T(128)} %clamp.3, (s32[1]{0:T(128)}) %tuple.15, (f32[1]{0:T(128)}) %tuple.16, () %tuple.14), branch_computations={%region_0.1_spmd, %region_1.2_spmd, %region_2.3_spmd} | conditional | bytes 8 | solution.py:218
  0.0 0.6 %branch_0_fun.1 = f32[1,128]{1,0:T(1,128)S(1)} custom-call(s32[1]{0:T(128)} %get-tuple-element.12.value), custom_call_target="tpu_custom_call" | custom-call | tf_op jit(solution)/shard_map/cond/branch_0_fun/pallas_call | solution.py:215
  0.7 9.1 %shard_map.90.share = f32[4,128]{1,0:T(4,128)S(1)} custom-call(f32[1,128]{1,0:T(1,128)S(1)} %get-tuple-element.15.given, f32[12,4,128]{2,1,0:T(4,128)} %leaf_hbm.1, f32[10,128]{1,0:T(8,128)} %soil_hbm.1, f32[4,10]{1,0:T(4,128)} %root_hbm.1, f32[4,4096]{1,0:T(4,128)} %weight_hbm.1, s32[1,4096]{1,0:T(1,128)} %bitcast.2, s32[1,4096]{1,0:T(1,128)} %bitcast.3), custom_call_target="tpu_custom_call" | custom-call | tf_op jit(solution)/shard_map/pallas_call | solution.py:228
  9.8 0.5 %shard_map.91 = f32[4,128]{1,0:T(4,128)} custom-call(f32[4,128]{1,0:T(4,128)S(1)} %shard_map.90.share), custom_call_target="tpu_custom_call" | custom-call | tf_op jit(solution)/shard_map/pallas_call | solution.py:250

commit v5 on v4

--- a/solution.py
+++ b/solution.py
@@ -56,14 +56,32 @@
     out[...] = jnp.zeros(out.shape, out.dtype)
 
 
-def put_rows(share, out, sem):
-    for i in range(share.shape[0]):
-        row = pl.ds(i, 1)
-        pltpu.make_async_copy(share.at[row], out.at[row], sem).start()
-    pltpu.make_async_copy(share, out, sem).wait()
+def put_rows(share, out):
+    def body(sem):
+        for i in range(share.shape[0]):
+            row = pl.ds(i, 1)
+            pltpu.make_async_copy(share.at[row], out.at[row], sem).start()
+        pltpu.make_async_copy(share, out, sem).wait()
+
+    pl.run_scoped(body, pltpu.SemaphoreType.DMA)
 
 
 def kernel(
+    n, m, given, leaf_hbm, soil_hbm, root_hbm, weight_hbm, owner_hbm, local_hbm,
+    out_ref, soil, root, weight, owner, local, leaf, scalars, sums, pairs, got,
+    tally, sum_sem, part_sem, met_sem,
+):
+    def body(load_sem, side_sem, root_sem, send_sem):
+        exchange(
+            n, m, given, leaf_hbm, soil_hbm, root_hbm, weight_hbm, owner_hbm, local_hbm,
+            out_ref, soil, root, weight, owner, local, leaf, scalars, sums, pairs, got,
+            tally, load_sem, side_sem, root_sem, send_sem, sum_sem, part_sem, met_sem,
+        )
+
+    pl.run_scoped(body, *[pltpu.SemaphoreType.DMA] * 4)
+
+
+def exchange(
     n, m, given, leaf_hbm, soil_hbm, root_hbm, weight_hbm, owner_hbm, local_hbm,
     out_ref, soil, root, weight, owner, local, leaf, scalars, sums, pairs, got,
     tally, load_sem, side_sem, root_sem, send_sem, sum_sem, part_sem, met_sem,
@@ -96,7 +114,7 @@
     peers = [lax.rem(layer + j, m) for j in range(1, m)]
     for k in peers:
         greet(barrier, blk, k)
-    for b in range(n):
+    for b in reversed(range(n)):
 
         @pl.when(blk != b)
         def _():
@@ -242,7 +260,7 @@
             pltpu.VMEM((m, 2, types, cells), f32),
             pltpu.VMEM((n, m, types, cells), f32),
             pltpu.VMEM((rows, cells), f32),
-            *[pltpu.SemaphoreType.DMA] * 6,
+            *[pltpu.SemaphoreType.DMA] * 2,
             pltpu.SemaphoreType.REGULAR,
         ],
         compiler_params=pltpu.CompilerParams(collective_id=0, has_side_effects=True),
@@ -252,7 +270,6 @@
         out_shape=jax.ShapeDtypeStruct(share.shape, f32),
         in_specs=[vmem],
         out_specs=hbm,
-        scratch_shapes=[pltpu.SemaphoreType.DMA],
     )(pltpu.with_memory_space_constraint(share, pltpu.VMEM))
 
 

time: 10.5 us -> 10.4 us (level)
  no operation moved by 1% of the time
where the time goes in v5:
time: 10.4 us; the launch traced here: 10.3 us
  Pallas kernels  10.2 us (98%)
    pallas_call x1, Pallas kernels, on_device(): pl.pallas_call(functools.partial(kernel, n, m), out_shape=pltpu.VMEM((typ...  9.06 us
    pallas_call x1, Pallas kernels, reader(): pl.pallas_call(spread, out_shape=row, in_specs=[smem], out_specs=vmem)  0.65 us
    pallas_call x1, Pallas kernels, on_device(): pl.pallas_call(put_rows, out_shape=jax.ShapeDtypeStruct(share.shape, f32)...  0.52 us

profile of v5, /device:TPU:0, one launch (start us, length us, event | category | flops | bytes accessed | tf_op | source)
XLA Modules:
  0.0 10.3 jit_solution(11555272918083749333)
XLA Ops:
  0.0 0.7 %conditional.1 = (f32[1,128]{1,0:T(1,128)S(1)}) conditional(s32[]{:T(128)} %clamp.3, (s32[1]{0:T(128)}) %tuple.15, (f32[1]{0:T(128)}) %tuple.16, () %tuple.14), branch_computations={%region_0.1_spmd, %region_1.2_spmd, %region_2.3_spmd} | conditional | bytes 8 | solution.py:236
  0.0 0.6 %branch_0_fun.1 = f32[1,128]{1,0:T(1,128)S(1)} custom-call(s32[1]{0:T(128)} %get-tuple-element.12.value), custom_call_target="tpu_custom_call" | custom-call | tf_op jit(solution)/shard_map/cond/branch_0_fun/pallas_call | solution.py:233
  0.7 9.1 %shard_map.90.share = f32[4,128]{1,0:T(4,128)S(1)} custom-call(f32[1,128]{1,0:T(1,128)S(1)} %get-tuple-element.15.given, f32[12,4,128]{2,1,0:T(4,128)} %leaf_hbm.1, f32[10,128]{1,0:T(8,128)} %soil_hbm.1, f32[4,10]{1,0:T(4,128)} %root_hbm.1, f32[4,4096]{1,0:T(4,128)} %weight_hbm.1, s32[1,4096]{1,0:T(1,128)} %bitcast.2, s32[1,4096]{1,0:T(1,128)} %bitcast.3), custom_call_target="tpu_custom_call" | custom-call | tf_op jit(solution)/shard_map/pallas_call | solution.py:246
  9.7 0.5 %shard_map.91 = f32[4,128]{1,0:T(4,128)} custom-call(f32[4,128]{1,0:T(4,128)S(1)} %shard_map.90.share), custom_call_target="tpu_custom_call" | custom-call | tf_op jit(solution)/shard_map/pallas_call | solution.py:268

commit v6 on v5

--- a/solution.py
+++ b/solution.py
@@ -96,15 +96,17 @@
     def settle(semaphore, rows):
         pltpu.make_async_copy(tally.at[pl.ds(0, rows)], tally.at[pl.ds(0, rows)], semaphore).wait()
 
-    for source, target, semaphore in (
-        (weight_hbm, weight, load_sem),
+    half = weight.shape[1] // 2
+    for i, (source, target, semaphore) in enumerate((
+        (weight_hbm.at[:, pl.ds(0, half)], weight.at[:, pl.ds(0, half)], load_sem),
+        (weight_hbm.at[:, pl.ds(half, half)], weight.at[:, pl.ds(half, half)], load_sem),
         (owner_hbm, owner, load_sem),
         (local_hbm, local, load_sem),
         (root_hbm, root, root_sem),
         (soil_hbm, soil, side_sem),
         (leaf_hbm, leaf.at[layer], side_sem),
-    ):
-        pltpu.make_async_copy(source, target, semaphore).start()
+    )):
+        pltpu.make_async_copy(source, target, semaphore).start(priority=i % 2)
 
     barrier = pltpu.get_barrier_semaphore()
 
@@ -152,19 +154,21 @@
 
     pl.semaphore_wait(barrier, jnp.where(is_near, m - 1, n * m - 1))
 
+    def send_sums(b):
+        for k in range(m):
+            send(sums.at[b], got.at[blk, layer], sum_sem, b, k)
+            if b == 0 and k >= NEAR:
+                greet(met_sem, b, k)
+
+    pl.when(blk != 0)(functools.partial(send_sums, 0))
+
     @pl.when(is_near)
     def _():
         send_peers()
         pl.semaphore_wait(met_sem, (n - 1) * m)
 
-    for b in range(n):
-
-        @pl.when(blk != b)
-        def _():
-            for k in range(m):
-                send(sums.at[b], got.at[blk, layer], sum_sem, b, k)
-                if b == 0 and k >= NEAR:
-                    greet(met_sem, b, k)
+    for b in range(1, n):
+        pl.when(blk != b)(functools.partial(send_sums, b))
 
     @pl.when(jnp.logical_not(is_near))
     def _():

time: 10.4 us -> 10.4 us (level)
  no operation moved by 1% of the time
where the time goes in v6:
time: 10.4 us; the launch traced here: 10.2 us
  Pallas kernels  10.2 us (98%)
    pallas_call x1, Pallas kernels, on_device(): pl.pallas_call(functools.partial(kernel, n, m), out_shape=pltpu.VMEM((typ...  9.04 us
    pallas_call x1, Pallas kernels, reader(): pl.pallas_call(spread, out_shape=row, in_specs=[smem], out_specs=vmem)  0.65 us
    pallas_call x1, Pallas kernels, on_device(): pl.pallas_call(put_rows, out_shape=jax.ShapeDtypeStruct(share.shape, f32)...  0.52 us

profile of v6, /device:TPU:0, one launch (start us, length us, event | category | flops | bytes accessed | tf_op | source)
XLA Modules:
  0.0 10.2 jit_solution(6462425373852415572)
XLA Ops:
  0.0 0.7 %conditional.1 = (f32[1,128]{1,0:T(1,128)S(1)}) conditional(s32[]{:T(128)} %clamp.3, (s32[1]{0:T(128)}) %tuple.15, (f32[1]{0:T(128)}) %tuple.16, () %tuple.14), branch_computations={%region_0.1_spmd, %region_1.2_spmd, %region_2.3_spmd} | conditional | bytes 8 | solution.py:240
  0.0 0.6 %branch_0_fun.1 = f32[1,128]{1,0:T(1,128)S(1)} custom-call(s32[1]{0:T(128)} %get-tuple-element.12.value), custom_call_target="tpu_custom_call" | custom-call | tf_op jit(solution)/shard_map/cond/branch_0_fun/pallas_call | solution.py:237
  0.7 9.0 %shard_map.90.share = f32[4,128]{1,0:T(4,128)S(1)} custom-call(f32[1,128]{1,0:T(1,128)S(1)} %get-tuple-element.15.given, f32[12,4,128]{2,1,0:T(4,128)} %leaf_hbm.1, f32[10,128]{1,0:T(8,128)} %soil_hbm.1, f32[4,10]{1,0:T(4,128)} %root_hbm.1, f32[4,4096]{1,0:T(4,128)} %weight_hbm.1, s32[1,4096]{1,0:T(1,128)} %bitcast.2, s32[1,4096]{1,0:T(1,128)} %bitcast.3), custom_call_target="tpu_custom_call" | custom-call | tf_op jit(solution)/shard_map/pallas_call | solution.py:250
  9.7 0.5 %shard_map.91 = f32[4,128]{1,0:T(4,128)} custom-call(f32[4,128]{1,0:T(4,128)S(1)} %shard_map.90.share), custom_call_target="tpu_custom_call" | custom-call | tf_op jit(solution)/shard_map/pallas_call | solution.py:272

commit v7 on v6

--- a/solution.py
+++ b/solution.py
@@ -204,8 +204,11 @@
     pl.when(is_reader)(lambda: settle(send_sem, sent + n * m - 1))
     pl.when(jnp.logical_not(is_reader))(lambda: settle(send_sem, sent))
     settle(sum_sem, (n - 1) * m * types)
-    for b in range(n):
-        grids = [grid + got[b, k] for k, grid in enumerate(grids)]
+    for k in range(m):
+        terms = [grids[k]] + [got[b, k] for b in range(n)]
+        while len(terms) > 1:
+            terms = [sum(terms[i + 1 : i + 2], terms[i]) for i in range(0, len(terms), 2)]
+        grids[k] = terms[0]
     mine, everyone = None, None
     for k in range(m):
         grid = grids[k] * effects[k]

time: 10.4 us -> 10.4 us (level)
  no operation moved by 1% of the time
where the time goes in v7:
time: 10.4 us; the launch traced here: 10.2 us
  Pallas kernels  10.2 us (98%)
    pallas_call x1, Pallas kernels, on_device(): pl.pallas_call(functools.partial(kernel, n, m), out_shape=pltpu.VMEM((typ...  9.04 us
    pallas_call x1, Pallas kernels, reader(): pl.pallas_call(spread, out_shape=row, in_specs=[smem], out_specs=vmem)  0.65 us
    pallas_call x1, Pallas kernels, on_device(): pl.pallas_call(put_rows, out_shape=jax.ShapeDtypeStruct(share.shape, f32)...  0.52 us

profile of v7, /device:TPU:0, one launch (start us, length us, event | category | flops | bytes accessed | tf_op | source)
XLA Modules:
  0.0 10.2 jit_solution(8381922951538251787)
XLA Ops:
  0.0 0.7 %conditional.1 = (f32[1,128]{1,0:T(1,128)S(1)}) conditional(s32[]{:T(128)} %clamp.3, (s32[1]{0:T(128)}) %tuple.15, (f32[1]{0:T(128)}) %tuple.16, () %tuple.14), branch_computations={%region_0.1_spmd, %region_1.2_spmd, %region_2.3_spmd} | conditional | bytes 8 | solution.py:243
  0.0 0.6 %branch_0_fun.1 = f32[1,128]{1,0:T(1,128)S(1)} custom-call(s32[1]{0:T(128)} %get-tuple-element.12.value), custom_call_target="tpu_custom_call" | custom-call | tf_op jit(solution)/shard_map/cond/branch_0_fun/pallas_call | solution.py:240
  0.7 9.0 %shard_map.90.share = f32[4,128]{1,0:T(4,128)S(1)} custom-call(f32[1,128]{1,0:T(1,128)S(1)} %get-tuple-element.15.given, f32[12,4,128]{2,1,0:T(4,128)} %leaf_hbm.1, f32[10,128]{1,0:T(8,128)} %soil_hbm.1, f32[4,10]{1,0:T(4,128)} %root_hbm.1, f32[4,4096]{1,0:T(4,128)} %weight_hbm.1, s32[1,4096]{1,0:T(1,128)} %bitcast.2, s32[1,4096]{1,0:T(1,128)} %bitcast.3), custom_call_target="tpu_custom_call" | custom-call | tf_op jit(solution)/shard_map/pallas_call | solution.py:253
  9.7 0.5 %shard_map.91 = f32[4,128]{1,0:T(4,128)} custom-call(f32[4,128]{1,0:T(4,128)S(1)} %shard_map.90.share), custom_call_target="tpu_custom_call" | custom-call | tf_op jit(solution)/shard_map/pallas_call | solution.py:275
